TPU v7x, 256 devices: a whole 4x4x8 slice. The times are simulated.
256 devices in a mesh: dp: 16 (over z_lo, x, core), tensor: 16 (over z_hi, y).
Axes of the slice: x: 4, y: 4, z: 8 (z_hi: 4, z_lo: 2; z = z_hi * 2 + z_lo), core: 2. Of those that a mesh axis runs over, the one named last changes fastest.
Arguments:
- activations: bfloat16 [4096, 5120], P('dp'), may hold values from -6 to 6
- grad_out: bfloat16 [4096, 5120], P('dp'), may hold values from -6 to 6
- gate_pre: bfloat16 [4096, 7168], P('dp', 'tensor'), may hold values from -8 to 8
- up_pre: bfloat16 [4096, 7168], P('dp', 'tensor'), may hold values from -6 to 6
- gate_up: bfloat16 [5120, 2, 7168], P('dp', None, 'tensor'), may hold values from -0.078125 to 0.078125
- down_weight: bfloat16 [5120, 7168], P('dp', 'tensor'), may hold values from -0.0625 to 0.0625
Outputs:
- grad_input: bfloat16 [4096, 5120], P('dp')
- grad_gate_up: float32 [5120, 2, 7168], P('dp', None, 'tensor')
- grad_down: float32 [5120, 7168], P('dp', 'tensor')
All inputs are finite; a program needn't handle non-finite values.
Results may differ from a plain program's by a relative error of at most 0.017.
Values may be sent and summed in bfloat16 or wider, within the bound.
No kernel may reach another device: no remote copies, remote signals or barrier semaphores. Data moves between devices by JAX's collectives and lax.ppermute only.
A program may use at most 128 MiB of HBM per device.

v0:
```python
import jax
import jax.numpy as jnp
from jax import lax
from jax.sharding import Mesh
from jax.sharding import PartitionSpec as P

DP = ("dp_0", "dp_1", "dp_2")
TENSOR = ("tensor_0", "tensor_1")


def sum_in_order(pieces, axes, order):
    dims = [lax.axis_size(a) for a in axes]
    pieces = pieces.reshape(*dims, *pieces.shape[1:])
    pieces = pieces.transpose(*order, *range(len(axes), pieces.ndim))
    pieces = pieces.reshape(-1, *pieces.shape[len(axes) :])
    for k in order:
        pieces = lax.psum_scatter(pieces, axes[k], scatter_dimension=0, tiled=True)
    return pieces[0]


def split_up(x, dim, devices):
    dims = x.shape
    pieces = x.reshape(*dims[:dim], devices, dims[dim] // devices, *dims[dim + 1 :])
    return jnp.moveaxis(pieces, dim, 0)


def sum_by_axis(x, axes, order, dim):
    devices = lax.axis_size(axes)
    return sum_in_order(split_up(x, dim, devices), axes, order)


def sum_at_owner(x, axis, dim):
    devices = lax.axis_size(axis)
    pieces = lax.all_to_all(split_up(x, dim, devices), axis, 0, 0, tiled=True)
    return jnp.sum(pieces.astype(jnp.float32), axis=0)


def sum_in_two_steps(x, axes, dim):
    far, near = axes
    own = sum_at_owner(split_up(x, dim, lax.axis_size(far)), near, dim + 1)
    return jnp.sum(
        lax.all_to_all(own.astype(jnp.bfloat16), far, 0, 0, tiled=True).astype(jnp.float32), axis=0
    )


def per_device(activations, grad_out, gate_pre, up_pre, gate_up, down_weight):
    tokens = activations.shape[0]
    hidden_width = down_weight.shape[1]
    dp_count = lax.axis_size(DP)
    slab_rows = down_weight.shape[0]
    gate_wide = gate_pre.astype(jnp.float32)
    up_wide = up_pre.astype(jnp.float32)
    gate_sigmoid = jax.nn.sigmoid(gate_wide)
    gate_silu = gate_wide * gate_sigmoid
    hidden = (gate_silu * up_wide).astype(jnp.bfloat16)
    grad_h = jnp.dot(
        grad_out,
        lax.all_gather(down_weight, DP, axis=0, tiled=True),
        preferred_element_type=jnp.float32,
    )
    grad_gate = grad_h * up_wide * gate_sigmoid * (1.0 + gate_wide * (1.0 - gate_sigmoid))
    grad_up = grad_h * gate_silu
    grad_hidden = (
        jnp.stack([grad_gate, grad_up], axis=1)
        .astype(jnp.bfloat16)
        .reshape(tokens, 2 * hidden_width)
    )
    pieces = lax.all_gather(gate_up, DP, axis=0, tiled=True)
    flattened = pieces.reshape(pieces.shape[0], 2 * hidden_width)
    partial_sum = lax.dot_general(
        grad_hidden, flattened, (((1,), (1,)), ((), ())), preferred_element_type=jnp.float32
    )
    share_block = sum_by_axis(partial_sum.astype(jnp.bfloat16), TENSOR, (1, 0), 0).astype(
        jnp.float32
    )
    grad_input = lax.all_gather(share_block.astype(jnp.bfloat16), TENSOR, axis=0, tiled=True)
    gate_part = lax.dot_general(
        activations, grad_hidden, (((0,), (0,)), ((), ())), preferred_element_type=jnp.float32
    )
    down_part = lax.dot_general(
        grad_out, hidden, (((0,), (0,)), ((), ())), preferred_element_type=jnp.float32
    )
    summed = sum_in_two_steps(
        jnp.concatenate([gate_part, down_part], axis=1).astype(jnp.bfloat16),
        (("dp_0", "dp_1"), "dp_2"),
        0,
    )
    summed = summed / dp_count
    grad_gate_up = summed[:, : 2 * hidden_width].reshape(slab_rows, 2, hidden_width)
    grad_down = summed[:, 2 * hidden_width :]
    return (grad_input, grad_gate_up, grad_down)


def solution(mesh):
    split = Mesh(
        mesh.devices.reshape(2, 4, 2, 4, 4), ("dp_0", "dp_1", "dp_2", "tensor_0", "tensor_1")
    )
    return jax.shard_map(
        per_device,
        mesh=split,
        in_specs=(
            P(DP, None),
            P(DP, None),
            P(DP, TENSOR),
            P(DP, TENSOR),
            P(DP, None, TENSOR),
            P(DP, TENSOR),
        ),
        out_specs=(P(DP, None), P(DP, None, TENSOR), P(DP, TENSOR)),
        check_vma=False,
    )
```

profile of v0, /device:TPU:1, one launch (start us, length us, event | category | flops | bytes accessed | tf_op | source)
XLA Modules:
  0.0 286.9 jit_solution(15581350529174634229)
XLA Ops:
  7.2 0.0 all-gather.5.cloned.1.call-start
  7.2 0.7 all-gather.5.cloned.1.call-update
  7.9 0.0 all-gather.7.cloned.1.call-start
  8.0 2.0 copy.20
  10.0 0.0 all-gather.7.cloned.1.call-update
  10.0 5.5 %fusion = bf16[5120,448]{0,1:T(8,128)(2,1)} fusion(bf16[256,5120]{1,0:T(8,128)(2,1)} %param.7, bf16[256,448]{0,1:T(8,128)(2,1)} %param.9, bf16[256,448]{0,1:T(8,128)(2,1)} %param.8), kind=kOutput, calls=%fused_computation.5 | convolution fusion | flops 1177616384 | bytes 7667712 | tf_op jit(solution)/shard_map/dot_general | solution.py:80
  15.5 7.7 %copy.23 = bf16[5120,448]{1,0:T(8,128)(2,1)} copy(bf16[5120,448]{0,1:T(8,128)(2,1)} %fusion) | data formatting | bytes 9175040 | tf_op jit(solution)/shard_map/dot_general | solution.py:80
  23.1 32.7 %all-gather.5.cloned.1.call-done = bf16[5120,448]{1,0:T(8,128)(2,1)} async-done(((bf16[320,448]{1,0:T(8,128)(2,1)}), bf16[5120,448]{1,0:T(8,128)(2,1)}) %all-gather.5.cloned.1.call-update) | async-done | bytes 4587536 | tf_op jit(solution)/shard_map/all_gather | solution.py:58
  55.8 5.4 %fusion.4 = (bf16[256,1,448]{0,2,1:T(8,128)(2,1)S(1)}, bf16[256,1,448]{0,2,1:T(8,128)(2,1)S(1)}) fusion(bf16[256,448]{0,1:T(8,128)(2,1)S(1)} %copy-done.2, bf16[256,448]{0,1:T(8,128)(2,1)S(1)} %copy-done.3, bf16[256,5120]{1,0:T(8,128)(2,1)} %param.7, bf16[5120,448]{1,0:T(8,128)(2,1)} %all-gather.5.cloned.1.call-done), kind=kOutput, calls=%fused_computation.16 | convolution fusion | flops 1176125440 | bytes 8126464 | tf_op jit(solution)/shard_map/dot_general | solution.py:56
  61.3 6.0 %convert_bitcast_fusion = bf16[5120,896]{0,1:T(8,128)(2,1)} fusion(bf16[256,896]{0,1:T(8,128)(2,1)S(1)} %bitcast.33, bf16[256,5120]{1,0:T(8,128)(2,1)S(1)} %copy-done), kind=kOutput, calls=%fused_computation.2 | convolution fusion | flops 2353397760 | bytes 12255232 | tf_op jit(solution)/shard_map/dot_general | solution.py:77
  67.3 12.9 %copy.22 = bf16[5120,896]{1,0:T(8,128)(2,1)} copy(bf16[5120,896]{0,1:T(8,128)(2,1)} %convert_bitcast_fusion) | data formatting | bytes 18350080 | tf_op jit(solution)/shard_map/dot_general | solution.py:77
  80.2 7.7 %maximum_bitcast_fusion = bf16[2,8,320,1344]{3,2,0,1:T(8,128)(2,1)S(1)} fusion(bf16[8,2,320,448]{3,2,1,0:T(8,128)(2,1)} %bitcast.29, bf16[8,2,320,896]{3,2,1,0:T(8,128)(2,1)} %bitcast.28), kind=kLoop, calls=%fused_computation | loop fusion | flops 27525120 | bytes 27525120 | tf_op jit(solution)/shard_map/transpose | solution.py:24
  87.9 3.6 %copy.24 = bf16[2,8,320,1344]{3,2,1,0:T(8,128)(2,1)S(1)} copy(bf16[2,8,320,1344]{3,2,0,1:T(8,128)(2,1)S(1)} %maximum_bitcast_fusion) | data formatting | bytes 27525120 | tf_op jit(solution)/shard_map/transpose | solution.py:24
  91.5 18.7 %all_to_all.10 = bf16[2,8,320,1344]{3,2,1,0:T(8,128)(2,1)} all-to-all(bf16[2,8,320,1344]{3,2,1,0:T(8,128)(2,1)S(1)} %copy.24), channel_id=1, replica_groups=mesh['dp_0'=2,'dp_1'=4,'dp_2'=2,'tensor_0'=4,'tensor_1'=4] {'dp_2'}, dimensions={0} | all-to-all | bytes 27525120 | tf_op jit(solution)/shard_map/all_to_all | solution.py:34
  110.2 13.1 %reduce_sum.21 = bf16[8,320,1344]{2,1,0:T(8,128)(2,1)} reduce(bf16[2,8,320,1344]{3,2,1,0:T(8,128)(2,1)} %all_to_all.10, bf16[]{:T(256)} %constant.6.clone.1), dimensions={0}, to_apply=%region_2.0 | reduce | flops 3440640 | bytes 20643842 | tf_op jit(solution)/shard_map/reduce_sum | solution.py:35
  123.3 4.8 %all-to-all-start.1 = ((bf16[8,320,1344]{2,1,0:T(8,128)(2,1)}), bf16[8,320,1344]{2,1,0:T(8,128)(2,1)}, u32[]{:S(2)}, u32[]{:S(2)}) async-start(bf16[8,320,1344]{2,1,0:T(8,128)(2,1)} %reduce_sum.21), calls=%async_computation.3 | async-start | bytes 14417920 | tf_op jit(solution)/shard_map/all_to_all | solution.py:42
  128.2 0.2 reduce-scatter.3.cloned.1.call-start
  128.4 0.0 all-gather.7.cloned.1.call-done
  128.4 11.1 %fusion.1 = bf16[256,5120]{1,0:T(8,128)(2,1)S(1)} fusion(bf16[5120,2,448]{2,0,1:T(8,128)(2,1)} %all-gather.7.cloned.1.call-done, bf16[256,1,448]{0,2,1:T(8,128)(2,1)S(1)} %get-tuple-element.4, bf16[256,1,448]{0,2,1:T(8,128)(2,1)S(1)} %get-tuple-element.3), kind=kOutput, calls=%fused_computation.6 | convolution fusion | flops 2350350336 | bytes 12255232 | tf_op jit(solution)/shard_map/dot_general | solution.py:70
  139.5 1.7 copy.21
  141.3 0.0 reduce-scatter.5.cloned.1.call-start
  141.3 37.2 %reduce-scatter.3.cloned.1.call-done = bf16[4,16,5120]{2,1,0:T(8,128)(2,1)} async-done(((bf16[16,16,5120]{2,1,0:T(8,128)(2,1)}), bf16[4,16,5120]{2,1,0:T(8,128)(2,1)}) %reduce-scatter.3.cloned.1.call-update) | async-done | bytes 655376 | tf_op jit(solution)/shard_map/reduce_scatter | solution.py:17
  178.5 0.0 all-gather.9.cloned.1.call-start
  178.6 34.9 %reduce-scatter.5.cloned.1.call-done = bf16[1,16,5120]{2,1,0:T(8,128)(2,1)} async-done(((bf16[4,16,5120]{2,1,0:T(8,128)(2,1)}), bf16[1,16,5120]{2,1,0:T(8,128)(2,1)}) %reduce-scatter.5.cloned.1.call-update) | async-done | bytes 163856 | tf_op jit(solution)/shard_map/reduce_scatter | solution.py:17
  213.5 4.7 %all-to-all-done.1 = bf16[8,320,1344]{2,1,0:T(8,128)(2,1)} async-done(((bf16[8,320,1344]{2,1,0:T(8,128)(2,1)}), bf16[8,320,1344]{2,1,0:T(8,128)(2,1)}, u32[]{:S(2)}, u32[]{:S(2)}) %all-to-all-start.1) | async-done | bytes 6881312 | tf_op jit(solution)/shard_map/all_to_all | solution.py:42
  218.2 4.3 %convert_reduce_fusion = f32[320,1344]{1,0:T(8,128)S(1)} fusion(bf16[8,320,1344]{2,1,0:T(8,128)(2,1)} %all-to-all-done.1), kind=kLoop, calls=%fused_computation.1 | loop fusion | flops 6451200 | bytes 8601600 | tf_op jit(solution)/shard_map/reduce_sum | solution.py:41
  222.5 0.1 broadcast_multiply_fusion
  222.6 1.1 slice.8
  223.7 0.9 slice.9
  224.6 3.5 %reshape.21 = f32[320,2,448]{2,1,0:T(2,128)} reshape(f32[320,896]{1,0:T(8,128)} %slice.8) | data formatting | bytes 2293760 | tf_op jit(solution)/shard_map/reshape | solution.py:89
  228.1 48.9 %all-gather.9.cloned.1.call-done = bf16[1,256,5120]{2,1,0:T(8,128)(2,1)} async-done(((bf16[1,16,5120]{2,1,0:T(8,128)(2,1)}), bf16[1,256,5120]{2,1,0:T(8,128)(2,1)}) %all-gather.9.cloned.1.call-update) | async-done | bytes 2621456 | tf_op jit(solution)/shard_map/all_gather | solution.py:76
  277.0 3.4 %copy.26 = bf16[256,5120]{1,0:T(8,128)(2,1)} copy(bf16[256,5120]{1,0:T(8,128)(2,1)} %bitcast.31) | data formatting | bytes 5242880
  (12 shorter events, 0.1 us)
Async XLA Ops:
  7.2 54.1 %copy-start = (bf16[256,5120]{1,0:T(8,128)(2,1)S(1)}, bf16[256,5120]{1,0:T(8,128)(2,1)}, u32[]{:S(2)}) copy-start(bf16[256,5120]{1,0:T(8,128)(2,1)} %param.6) | copy-start | bytes 7864324
  7.2 48.6 %all-gather.5.cloned.1.call-start = ((), (), s32[]{:S(2)}) async-start(), calls=%async_computation.4 | async-start | bytes 5570560 | tf_op jit(solution)/shard_map/all_gather | solution.py:58
  7.9 120.5 %all-gather.7.cloned.1.call-start = ((), (), s32[]{:S(2)}) async-start(), calls=%async_computation.5 | async-start | bytes 11141120 | tf_op jit(solution)/shard_map/all_gather | solution.py:68
  15.5 40.4 %copy-start.2 = (bf16[256,448]{0,1:T(8,128)(2,1)S(1)}, bf16[256,448]{0,1:T(8,128)(2,1)}, u32[]{:S(2)}) copy-start(bf16[256,448]{0,1:T(8,128)(2,1)} %param.9) | copy-start | bytes 688132
  15.5 40.4 %copy-start.3 = (bf16[256,448]{0,1:T(8,128)(2,1)S(1)}, bf16[256,448]{0,1:T(8,128)(2,1)}, u32[]{:S(2)}) copy-start(bf16[256,448]{0,1:T(8,128)(2,1)} %param.8) | copy-start | bytes 688132
  123.3 94.9 %all-to-all-start.1 = ((bf16[8,320,1344]{2,1,0:T(8,128)(2,1)}), bf16[8,320,1344]{2,1,0:T(8,128)(2,1)}, u32[]{:S(2)}, u32[]{:S(2)}) async-start(bf16[8,320,1344]{2,1,0:T(8,128)(2,1)} %reduce_sum.21), calls=%async_computation.3 | async-start | bytes 14417920 | tf_op jit(solution)/shard_map/all_to_all | solution.py:42
  128.2 50.3 %reduce-scatter.3.cloned.1.call-start = ((), (), s32[]{:S(2)}) async-start(), calls=%async_computation.6 | async-start | bytes 3276800 | tf_op jit(solution)/shard_map/reduce_scatter | solution.py:17
  141.3 72.2 %reduce-scatter.5.cloned.1.call-start = ((), (), s32[]{:S(2)}) async-start(), calls=%async_computation.7 | async-start | bytes 819200 | tf_op jit(solution)/shard_map/reduce_scatter | solution.py:17
  178.5 98.5 %all-gather.9.cloned.1.call-start = ((), (), s32[]{:S(2)}) async-start(), calls=%async_computation.8 | async-start | bytes 2785280 | tf_op jit(solution)/shard_map/all_gather | solution.py:76
  222.5 57.9 %copy-start.1 = (bf16[256,5120]{1,0:T(8,128)(2,1)S(1)}, bf16[256,5120]{1,0:T(8,128)(2,1)}, u32[]{:S(2)}) copy-start(bf16[256,5120]{1,0:T(8,128)(2,1)} %param.6) | copy-start | bytes 7864324
Sparse Core Ops, SparseCore 0:
  9.8 45.9 all-gather.4
  58.2 64.2 all-gather.6
  141.4 37.0 reduce-scatter.2
  180.9 32.5 reduce-scatter.4
  215.8 61.1 all-gather.8
where the time goes:
time: 288 us; the launch traced here: 287 us
  waiting for transfers between devices  159 us (55%)
  local copies, waits for them, and re-layouts  36.8 us (13%)
  matrix products  28 us (10%)
  other arithmetic  25.3 us (9%)
  blocking collectives  18.7 us (6%)
  between operations  13.9 us (5%)
  starting transfers between devices  5.22 us (2%)
    reduce_scatter x2, waiting for transfers between devices, sum_in_order(): pieces = lax.psum_scatter(pieces, axes[k], scatter_dimension=0, tiled=True)  72.1 us
    all_gather x1, waiting for transfers between devices, per_device(): lax.all_gather(share_block.astype(jnp.bfloat16), TENSOR, axis=0, tiled=True)  48.9 us
    all_gather x1, waiting for transfers between devices, per_device(): lax.all_gather(down_weight, DP, axis=0, tiled=True)  32.7 us
    all_to_all x1, blocking collectives, sum_at_owner(): pieces = lax.all_to_all(split_up(x, dim, devices), axis, 0, 0, tiled=True)  18.7 us
    reduce_sum x1, other arithmetic, sum_at_owner(): return jnp.sum(pieces.astype(jnp.float32), axis=0)  13.1 us
    dot_general x1, local copies, waits for them, and re-layouts, per_device(): lax.dot_general(activations, grad_hidden, (((0,), (0,)), ((), ())), prefe...  12.9 us
    dot_general x1, matrix products, per_device(): lax.dot_general(grad_hidden, flattened, (((1,), (1,)), ((), ())), preferr...  11.1 us
    transpose x1, other arithmetic, split_up(): return jnp.moveaxis(pieces, dim, 0)  7.67 us
  transfers between devices with their start and end apart: 6, of which 5 were waited for; matrix products, arithmetic and copies ran while one was open for 30% of the time, Pallas kernels for 0%

commit v1 on v0

--- a/solution.py
+++ b/solution.py
@@ -73,7 +73,12 @@
     share_block = sum_by_axis(partial_sum.astype(jnp.bfloat16), TENSOR, (1, 0), 0).astype(
         jnp.float32
     )
-    grad_input = lax.all_gather(share_block.astype(jnp.bfloat16), TENSOR, axis=0, tiled=True)
+    grad_input = jnp.concatenate(
+        lax.all_to_all(
+            jnp.stack([share_block.astype(jnp.bfloat16)] * lax.axis_size(TENSOR)), TENSOR, 0, 0
+        ),
+        axis=0,
+    )
     gate_part = lax.dot_general(
         activations, grad_hidden, (((0,), (0,)), ((), ())), preferred_element_type=jnp.float32
     )

time: 288 us -> 306 us (1.062)
  starting transfers between devices: 5.22 us -> 13.8 us
  waiting for transfers between devices: 159 us -> 164 us
    all_to_all x0 -> x1, waiting for transfers between devices: none -> 54.2 us  [per_device(): lax.all_to_all(jnp.stack([share_block.astype(jnp.bfloat16)] * lax.axis_si...]
    all_gather x1 -> x0, waiting for transfers between devices: 48.9 us -> none  [per_device(): lax.all_gather(share_block.astype(jnp.bfloat16), TENSOR, axis=0, tiled=True)]
    all_to_all x1, waiting for transfers between devices: 4.67 us -> 39.7 us  [sum_in_two_steps(): lax.all_to_all(own.astype(jnp.bfloat16), far, 0, 0, tiled=True)]
    reduce_scatter x2, waiting for transfers between devices: 72.1 us -> 37.2 us  [sum_in_order(): pieces = lax.psum_scatter(pieces, axes[k], scatter_dimension=0, tiled=True)]
    all_to_all x0 -> x1, starting transfers between devices: none -> 8.63 us  [per_device(): lax.all_to_all(jnp.stack([share_block.astype(jnp.bfloat16)] * lax.axis_si...]
    another operation x0 -> x2, local copies, waits for them, and re-layouts: none -> 4.43 us  [the longest x1 2.7 us: per_device(): jnp.stack([share_block.astype(jnp.bfloat16)] * lax.axis_size(TENSOR))]
  transfers between devices with their start and end apart: 6 -> 6, of which waited for: 5 -> 4; matrix products, arithmetic and copies ran while one was open for 30% -> 29% of each run, Pallas kernels for 0% -> 0%
where the time goes in v1:
time: 306 us; the launch traced here: 304 us
  waiting for transfers between devices  164 us (54%)
  local copies, waits for them, and re-layouts  39.6 us (13%)
  matrix products  28 us (9%)
  other arithmetic  25.3 us (8%)
  blocking collectives  18.7 us (6%)
  between operations  13.9 us (5%)
  starting transfers between devices  13.8 us (5%)
    all_to_all x1, waiting for transfers between devices, per_device(): lax.all_to_all(jnp.stack([share_block.astype(jnp.bfloat16)] * lax.axis_si...  54.2 us
    all_to_all x1, waiting for transfers between devices, sum_in_two_steps(): lax.all_to_all(own.astype(jnp.bfloat16), far, 0, 0, tiled=True)  39.7 us
    reduce_scatter x2, waiting for transfers between devices, sum_in_order(): pieces = lax.psum_scatter(pieces, axes[k], scatter_dimension=0, tiled=True)  37.2 us
    all_gather x1, waiting for transfers between devices, per_device(): lax.all_gather(down_weight, DP, axis=0, tiled=True)  32.6 us
    all_to_all x1, blocking collectives, sum_at_owner(): pieces = lax.all_to_all(split_up(x, dim, devices), axis, 0, 0, tiled=True)  18.7 us
    reduce_sum x1, other arithmetic, sum_at_owner(): return jnp.sum(pieces.astype(jnp.float32), axis=0)  13.1 us
    dot_general x1, local copies, waits for them, and re-layouts, per_device(): lax.dot_general(activations, grad_hidden, (((0,), (0,)), ((), ())), prefe...  12.8 us
    dot_general x1, matrix products, per_device(): lax.dot_general(grad_hidden, flattened, (((1,), (1,)), ((), ())), preferr...  11.1 us
  transfers between devices with their start and end apart: 6, of which 4 were waited for; matrix products, arithmetic and copies ran while one was open for 29% of the time, Pallas kernels for 0%

profile of v1, /device:TPU:1, one launch (start us, length us, event | category | flops | bytes accessed | tf_op | source)
XLA Modules:
  0.0 303.6 jit_solution(14931602729919223324)
XLA Ops:
  7.2 0.0 all-gather.3.cloned.1.call-start
  7.2 0.7 all-gather.3.cloned.1.call-update
  7.9 0.0 all-gather.5.cloned.1.call-start
  8.0 2.0 copy.19
  10.0 0.0 all-gather.5.cloned.1.call-update
  10.0 5.5 %fusion = bf16[5120,448]{0,1:T(8,128)(2,1)} fusion(bf16[256,5120]{1,0:T(8,128)(2,1)} %param.7, bf16[256,448]{0,1:T(8,128)(2,1)} %param.9, bf16[256,448]{0,1:T(8,128)(2,1)} %param.8), kind=kOutput, calls=%fused_computation.5 | convolution fusion | flops 1177616384 | bytes 7667712 | tf_op jit(solution)/shard_map/dot_general | solution.py:85
  15.5 7.7 %copy.22 = bf16[5120,448]{1,0:T(8,128)(2,1)} copy(bf16[5120,448]{0,1:T(8,128)(2,1)} %fusion) | data formatting | bytes 9175040 | tf_op jit(solution)/shard_map/dot_general | solution.py:85
  23.2 32.6 %all-gather.3.cloned.1.call-done = bf16[5120,448]{1,0:T(8,128)(2,1)} async-done(((bf16[320,448]{1,0:T(8,128)(2,1)}), bf16[5120,448]{1,0:T(8,128)(2,1)}) %all-gather.3.cloned.1.call-update) | async-done | bytes 4587536 | tf_op jit(solution)/shard_map/all_gather | solution.py:58
  55.8 5.4 %fusion.4 = (bf16[256,1,448]{0,2,1:T(8,128)(2,1)S(1)}, bf16[256,1,448]{0,2,1:T(8,128)(2,1)S(1)}) fusion(bf16[256,448]{0,1:T(8,128)(2,1)S(1)} %copy-done.2, bf16[256,448]{0,1:T(8,128)(2,1)S(1)} %copy-done.3, bf16[256,5120]{1,0:T(8,128)(2,1)} %param.7, bf16[5120,448]{1,0:T(8,128)(2,1)} %all-gather.3.cloned.1.call-done), kind=kOutput, calls=%fused_computation.16 | convolution fusion | flops 1176125440 | bytes 8126464 | tf_op jit(solution)/shard_map/dot_general | solution.py:56
  61.3 6.0 %convert_bitcast_fusion = bf16[5120,896]{0,1:T(8,128)(2,1)} fusion(bf16[256,896]{0,1:T(8,128)(2,1)S(1)} %bitcast.33, bf16[256,5120]{1,0:T(8,128)(2,1)S(1)} %copy-done), kind=kOutput, calls=%fused_computation.2 | convolution fusion | flops 2353397760 | bytes 12255232 | tf_op jit(solution)/shard_map/dot_general | solution.py:82
  67.3 12.8 %copy.21 = bf16[5120,896]{1,0:T(8,128)(2,1)} copy(bf16[5120,896]{0,1:T(8,128)(2,1)} %convert_bitcast_fusion) | data formatting | bytes 18350080 | tf_op jit(solution)/shard_map/dot_general | solution.py:82
  80.1 7.7 %maximum_bitcast_fusion = bf16[2,8,320,1344]{3,2,0,1:T(8,128)(2,1)S(1)} fusion(bf16[8,2,320,448]{3,2,1,0:T(8,128)(2,1)} %bitcast.30, bf16[8,2,320,896]{3,2,1,0:T(8,128)(2,1)} %bitcast.29), kind=kLoop, calls=%fused_computation | loop fusion | flops 27525120 | bytes 27525120 | tf_op jit(solution)/shard_map/transpose | solution.py:24
  87.8 3.6 %copy.23 = bf16[2,8,320,1344]{3,2,1,0:T(8,128)(2,1)S(1)} copy(bf16[2,8,320,1344]{3,2,0,1:T(8,128)(2,1)S(1)} %maximum_bitcast_fusion) | data formatting | bytes 27525120 | tf_op jit(solution)/shard_map/transpose | solution.py:24
  91.5 18.7 %all_to_all.15 = bf16[2,8,320,1344]{3,2,1,0:T(8,128)(2,1)} all-to-all(bf16[2,8,320,1344]{3,2,1,0:T(8,128)(2,1)S(1)} %copy.23), channel_id=1, replica_groups=mesh['dp_0'=2,'dp_1'=4,'dp_2'=2,'tensor_0'=4,'tensor_1'=4] {'dp_2'}, dimensions={0} | all-to-all | bytes 27525120 | tf_op jit(solution)/shard_map/all_to_all | solution.py:34
  110.2 13.1 %reduce_sum.21 = bf16[8,320,1344]{2,1,0:T(8,128)(2,1)} reduce(bf16[2,8,320,1344]{3,2,1,0:T(8,128)(2,1)} %all_to_all.15, bf16[]{:T(256)} %constant.6.clone.1), dimensions={0}, to_apply=%region_2.0 | reduce | flops 3440640 | bytes 20643842 | tf_op jit(solution)/shard_map/reduce_sum | solution.py:35
  123.3 4.8 %all-to-all-start.2 = ((bf16[8,320,1344]{2,1,0:T(8,128)(2,1)}), bf16[8,320,1344]{2,1,0:T(8,128)(2,1)}, u32[]{:S(2)}, u32[]{:S(2)}) async-start(bf16[8,320,1344]{2,1,0:T(8,128)(2,1)} %reduce_sum.21), calls=%async_computation.4 | async-start | bytes 14417920 | tf_op jit(solution)/shard_map/all_to_all | solution.py:42
  128.2 0.2 reduce-scatter.3.cloned.1.call-start
  128.4 0.0 all-gather.5.cloned.1.call-done
  128.4 11.1 %fusion.1 = bf16[256,5120]{1,0:T(8,128)(2,1)S(1)} fusion(bf16[5120,2,448]{2,0,1:T(8,128)(2,1)} %all-gather.5.cloned.1.call-done, bf16[256,1,448]{0,2,1:T(8,128)(2,1)S(1)} %get-tuple-element.4, bf16[256,1,448]{0,2,1:T(8,128)(2,1)S(1)} %get-tuple-element.3), kind=kOutput, calls=%fused_computation.6 | convolution fusion | flops 2350350336 | bytes 12255232 | tf_op jit(solution)/shard_map/dot_general | solution.py:70
  139.5 1.7 copy.20
  141.3 0.0 reduce-scatter.5.cloned.1.call-start
  141.3 37.2 %reduce-scatter.3.cloned.1.call-done = bf16[4,16,5120]{2,1,0:T(8,128)(2,1)} async-done(((bf16[16,16,5120]{2,1,0:T(8,128)(2,1)}), bf16[4,16,5120]{2,1,0:T(8,128)(2,1)}) %reduce-scatter.3.cloned.1.call-update) | async-done | bytes 655376 | tf_op jit(solution)/shard_map/reduce_scatter | solution.py:17
  178.5 39.7 %all-to-all-done.2 = bf16[8,320,1344]{2,1,0:T(8,128)(2,1)} async-done(((bf16[8,320,1344]{2,1,0:T(8,128)(2,1)}), bf16[8,320,1344]{2,1,0:T(8,128)(2,1)}, u32[]{:S(2)}, u32[]{:S(2)}) %all-to-all-start.2) | async-done | bytes 6881312 | tf_op jit(solution)/shard_map/all_to_all | solution.py:42
  218.2 2.7 stack.14
  220.9 8.6 %all-to-all-start = ((bf16[16,16,5120]{2,1,0:T(8,128)(2,1)}), bf16[16,16,5120]{2,1,0:T(8,128)(2,1)}, u32[]{:S(2)}, u32[]{:S(2)}) async-start(bf16[16,16,5120]{2,1,0:T(8,128)(2,1)} %stack.14), calls=%async_computation.2 | async-start | bytes 5242880 | tf_op jit(solution)/shard_map/all_to_all | solution.py:77
  229.5 4.3 %convert_reduce_fusion = f32[320,1344]{1,0:T(8,128)S(1)} fusion(bf16[8,320,1344]{2,1,0:T(8,128)(2,1)} %all-to-all-done.2), kind=kLoop, calls=%fused_computation.1 | loop fusion | flops 6451200 | bytes 8601600 | tf_op jit(solution)/shard_map/reduce_sum | solution.py:41
  233.8 0.1 broadcast_multiply_fusion
  234.0 1.1 slice.8
  235.0 0.9 slice.9
  236.0 3.5 %reshape.27 = f32[320,2,448]{2,1,0:T(2,128)} reshape(f32[320,896]{1,0:T(8,128)} %slice.8) | data formatting | bytes 2293760 | tf_op jit(solution)/shard_map/reshape | solution.py:94
  239.5 54.2 %all-to-all-done = bf16[16,16,5120]{2,1,0:T(8,128)(2,1)} async-done(((bf16[16,16,5120]{2,1,0:T(8,128)(2,1)}), bf16[16,16,5120]{2,1,0:T(8,128)(2,1)}, u32[]{:S(2)}, u32[]{:S(2)}) %all-to-all-start) | async-done | bytes 2621472 | tf_op jit(solution)/shard_map/all_to_all | solution.py:77
  293.6 3.4 %copy.25 = bf16[256,5120]{1,0:T(8,128)(2,1)} copy(bf16[256,5120]{1,0:T(8,128)(2,1)} %bitcast.7) | data formatting | bytes 5242880
  (12 shorter events, 0.1 us)
Async XLA Ops:
  7.2 54.1 %copy-start = (bf16[256,5120]{1,0:T(8,128)(2,1)S(1)}, bf16[256,5120]{1,0:T(8,128)(2,1)}, u32[]{:S(2)}) copy-start(bf16[256,5120]{1,0:T(8,128)(2,1)} %param.6) | copy-start | bytes 7864324
  7.2 48.6 %all-gather.3.cloned.1.call-start = ((), (), s32[]{:S(2)}) async-start(), calls=%async_computation.5 | async-start | bytes 5570560 | tf_op jit(solution)/shard_map/all_gather | solution.py:58
  7.9 120.5 %all-gather.5.cloned.1.call-start = ((), (), s32[]{:S(2)}) async-start(), calls=%async_computation.6 | async-start | bytes 11141120 | tf_op jit(solution)/shard_map/all_gather | solution.py:68
  15.5 40.4 %copy-start.2 = (bf16[256,448]{0,1:T(8,128)(2,1)S(1)}, bf16[256,448]{0,1:T(8,128)(2,1)}, u32[]{:S(2)}) copy-start(bf16[256,448]{0,1:T(8,128)(2,1)} %param.9) | copy-start | bytes 688132
  15.5 40.4 %copy-start.3 = (bf16[256,448]{0,1:T(8,128)(2,1)S(1)}, bf16[256,448]{0,1:T(8,128)(2,1)}, u32[]{:S(2)}) copy-start(bf16[256,448]{0,1:T(8,128)(2,1)} %param.8) | copy-start | bytes 688132
  123.3 94.9 %all-to-all-start.2 = ((bf16[8,320,1344]{2,1,0:T(8,128)(2,1)}), bf16[8,320,1344]{2,1,0:T(8,128)(2,1)}, u32[]{:S(2)}, u32[]{:S(2)}) async-start(bf16[8,320,1344]{2,1,0:T(8,128)(2,1)} %reduce_sum.21), calls=%async_computation.4 | async-start | bytes 14417920 | tf_op jit(solution)/shard_map/all_to_all | solution.py:42
  128.2 50.3 %reduce-scatter.3.cloned.1.call-start = ((), (), s32[]{:S(2)}) async-start(), calls=%async_computation.7 | async-start | bytes 3276800 | tf_op jit(solution)/shard_map/reduce_scatter | solution.py:17
  141.3 76.9 %reduce-scatter.5.cloned.1.call-start = ((), (), s32[]{:S(2)}) async-start(), calls=%async_computation.8 | async-start | bytes 819200 | tf_op jit(solution)/shard_map/reduce_scatter | solution.py:17
  220.9 72.8 %all-to-all-start = ((bf16[16,16,5120]{2,1,0:T(8,128)(2,1)}), bf16[16,16,5120]{2,1,0:T(8,128)(2,1)}, u32[]{:S(2)}, u32[]{:S(2)}) async-start(bf16[16,16,5120]{2,1,0:T(8,128)(2,1)} %stack.14), calls=%async_computation.2 | async-start | bytes 5242880 | tf_op jit(solution)/shard_map/all_to_all | solution.py:77
  233.8 63.2 %copy-start.1 = (bf16[256,5120]{1,0:T(8,128)(2,1)S(1)}, bf16[256,5120]{1,0:T(8,128)(2,1)}, u32[]{:S(2)}) copy-start(bf16[256,5120]{1,0:T(8,128)(2,1)} %param.6) | copy-start | bytes 7864324
Sparse Core Ops, SparseCore 0:
  9.8 45.9 all-gather.2
  58.2 64.2 all-gather.4
  141.4 37.0 reduce-scatter.2
  180.9 32.5 reduce-scatter.4
